TPU v7x, 32 devices: a whole 2x2x4 slice. The times are simulated.
32 devices in a mesh: groups: 2 (over x), seq: 4 (over y, core), head: 4 (over z).
Axes of the slice: x: 2, y: 2, z: 4, core: 2. Of those that a mesh axis runs over, the one named last changes fastest.
Arguments:
- query: bfloat16 [32, 16, 1024], P('groups', None, 'head'), parts along dimension 0, may hold values from -6 to 6, as said below
- new_key: bfloat16 [32, 16, 1024], P('groups', None, 'head'), parts along dimension 0, may hold values from -6 to 6
- new_value: bfloat16 [32, 16, 1024], P('groups', None, 'head'), parts along dimension 0, may hold values from -6 to 6
- keys: bfloat16 [32, 4096, 1024], P('groups', 'seq', 'head'), parts along dimension 0, may hold values from -6 to 6, as said below
- values: bfloat16 [32, 4096, 1024], P('groups', 'seq', 'head'), parts along dimension 0, may hold values from -6 to 6
- lengths: int32 [32], P('groups'), parts along dimension 0, may hold values from 2 to 4096
- time_bucket: int32 [32, 4096], P('groups', 'seq'), parts along dimension 0, may hold values from 0 to 63
- action: int32 [32, 4096], P('groups', 'seq'), parts along dimension 0, may hold values from 0 to 15
- time_bias: float32 [64, 8], P(None, 'head'), may hold values from -0.25 to 0.25
- action_bias: float32 [16, 8], P(None, 'head'), may hold values from -0.25 to 0.25
- gate: bfloat16 [32, 16, 1024], P('groups', None, 'head'), parts along dimension 0, may hold values from -6 to 6
- norm_gain: float32 [1024], P('head'), may hold values from 0.1 to 1.9
- w_out: bfloat16 [1024, 1024], P('head'), may hold values from -0.1875 to 0.1875
Outputs:
- output: bfloat16 [32, 16, 1024], P(('groups', 'seq'), None, 'head'), parts along dimension 0
There are 2 independent parts, one for each index of `groups`. A program takes and returns all parts, laid end to end along the dimension named above; an argument that names none is the same for every part. Nothing has to cross between parts.
Inputs may be any that keep to these rules, and one draw needn't show every extreme that they name: `query`: queries of order one; some users' queries may be large and equal to some of their keys. `keys`: keys of order one.
All inputs are finite; a program needn't handle non-finite values.
Results may differ from a plain program's by a relative error of at most 0.0056.
Values sent between devices are 32-bit elements; how exact they have to be, the bound alone decides.
A program may use at most 64 MiB of HBM per device.

v0:
```python
import math

import jax
import jax.numpy as jnp
from jax import lax
from jax.sharding import PartitionSpec as P


def body(
    query,
    new_key,
    new_value,
    keys,
    values,
    lengths,
    time_bucket,
    action,
    time_bias,
    action_bias,
    gate,
    norm_gain,
    w_out,
):
    user_count, block_len, row_width = keys.shape
    cand_count = query.shape[1]
    head_count = time_bias.shape[1]
    head_size = row_width // head_count
    score_scale = 1.0 / math.sqrt(head_size)
    seq_count = lax.axis_size("seq")
    seq_rank = lax.axis_index("seq")
    query_heads = query.reshape(user_count, cand_count, head_count, head_size)
    key_heads = keys.reshape(user_count, block_len, head_count, head_size)
    value_heads = values.reshape(user_count, block_len, head_count, head_size)
    scores = (
        jnp.einsum("uchd,ushd->uchs", query_heads, key_heads, preferred_element_type=jnp.float32)
        * score_scale
    )
    bucket_onehot = (
        time_bucket[:, :, None] == jnp.arange(time_bias.shape[0], dtype=jnp.int32)[None, None, :]
    ).astype(jnp.float32)
    action_onehot = (
        action[:, :, None] == jnp.arange(action_bias.shape[0], dtype=jnp.int32)[None, None, :]
    ).astype(jnp.float32)
    biases = jnp.einsum("usb,bh->uhs", bucket_onehot, time_bias, precision=lax.Precision.HIGHEST)
    biases = biases + jnp.einsum(
        "usb,bh->uhs", action_onehot, action_bias, precision=lax.Precision.HIGHEST
    )
    scores = scores + biases[:, None]
    position = seq_rank * block_len + jnp.arange(block_len, dtype=jnp.int32)
    valid = position[None, None, None, :] < lengths[:, None, None, None]
    block_max = jnp.max(jnp.where(valid, scores, -1e30), axis=-1)
    weights = jnp.where(valid, jnp.exp(scores - block_max[..., None]), 0.0)
    block_sum = jnp.sum(weights, axis=-1)
    block_acc = jnp.einsum(
        "uchs,ushd->uchd",
        weights.astype(jnp.bfloat16),
        value_heads,
        preferred_element_type=jnp.float32,
    )
    local_users = user_count // seq_count
    first_user = seq_rank * local_users

    def own_rows(source):
        return lax.dynamic_slice_in_dim(source, first_user, local_users, 0)

    received = (
        lax.all_to_all(block_max[None], "seq", split_axis=1, concat_axis=0, tiled=True),
        lax.all_to_all(block_sum[None], "seq", split_axis=1, concat_axis=0, tiled=True),
        lax.all_to_all(block_acc[None], "seq", split_axis=1, concat_axis=0, tiled=True),
    )
    running_max = jnp.max(received[0], axis=0)
    factors = jnp.exp(received[0] - running_max[None])
    total = jnp.sum(factors * received[1], axis=0)
    accum = jnp.sum(factors[..., None] * received[2], axis=0)
    own_query = (
        own_rows(query).astype(jnp.float32).reshape(local_users, cand_count, head_count, head_size)
    )
    own_key = (
        own_rows(new_key)
        .astype(jnp.float32)
        .reshape(local_users, cand_count, head_count, head_size)
    )
    own_value = (
        own_rows(new_value)
        .astype(jnp.float32)
        .reshape(local_users, cand_count, head_count, head_size)
    )
    own_score = jnp.sum(own_query * own_key, axis=-1) * score_scale
    overall = jnp.maximum(running_max, own_score)
    past_factor = jnp.exp(running_max - overall)
    own_factor = jnp.exp(own_score - overall)
    attended = (past_factor[..., None] * accum + own_factor[..., None] * own_value) / (
        past_factor * total + own_factor
    )[..., None]
    local_squares = jnp.sum(jnp.square(attended), axis=(2, 3))
    full_width = row_width * lax.axis_size("head")
    gate_heads = (
        own_rows(gate).astype(jnp.float32).reshape(local_users, cand_count, head_count, head_size)
    )
    hidden = (attended * norm_gain.reshape(head_count, head_size) * jax.nn.silu(gate_heads)).astype(
        jnp.bfloat16
    )
    hidden = hidden.reshape(local_users * cand_count, row_width)
    partial_out = jnp.dot(hidden, w_out, preferred_element_type=jnp.float32).reshape(
        local_users, cand_count, -1
    )
    squares = lax.psum(local_squares, "head")
    projected = lax.psum_scatter(partial_out, "head", scatter_dimension=2, tiled=True)
    factor = 1.0 / jnp.sqrt(squares / full_width + 1e-06)
    return (projected * factor[:, :, None]).astype(jnp.bfloat16)


def solution(mesh):
    placed = (
        P("groups", None, "head"),
        P("groups", None, "head"),
        P("groups", None, "head"),
        P("groups", "seq", "head"),
        P("groups", "seq", "head"),
        P("groups"),
        P("groups", "seq"),
        P("groups", "seq"),
        P(None, "head"),
        P(None, "head"),
        P("groups", None, "head"),
        P("head"),
        P("head", None),
    )
    return jax.shard_map(
        body,
        mesh=mesh,
        in_specs=placed,
        out_specs=P(("groups", "seq"), None, "head"),
        check_vma=False,
    )
```

profile of v0, /device:TPU:0, one launch (start us, length us, event | category | flops | bytes accessed | tf_op | source)
XLA Modules:
  0.0 77.0 jit_solution(13217166976046112141)
XLA Ops:
  6.5 0.8 %broadcast_compare_fusion = pred[16,1024]{1,0:T(8,128)(4,1)S(1)} fusion(s32[1024]{0:T(1024)S(1)} %iota_add_fusion, s32[16]{0:T(128)} %param.18), kind=kLoop, calls=%fused_computation.49 | loop fusion | flops 16384 | bytes 20544 | tf_op jit(solution)/shard_map/lt | solution.py:50
  7.3 1.3 %fusion.24 = f32[16,1024,2]{1,2,0:T(2,128)S(1)} fusion(s32[16,1024]{1,0:T(8,128)} %param.20, f32[16,2]{0,1:T(2,128)} %param.22), kind=kOutput, calls=%fused_computation.26 | convolution fusion | flops 6553600 | bytes 196736 | tf_op jit(solution)/shard_map/usb,bh->uhs/dot_general | solution.py:45
  8.6 2.2 %fusion.17 = f32[16,2,1024]{2,1,0:T(2,128)S(1)} fusion(f32[16,1024,2]{1,2,0:T(2,128)S(1)} %fusion.24, s32[16,1024]{1,0:T(8,128)} %param.19, f32[64,2]{0,1:T(2,128)} %param.21), kind=kOutput, calls=%fused_computation.19 | convolution fusion | flops 26247168 | bytes 328192 | tf_op jit(solution)/shard_map/usb,bh->uhs/dot_general | solution.py:44
  10.8 5.8 %fusion.7 = (f32[16,16,2]{1,2,0:T(2,128)S(1)}, f32[16,2,1024,16]{2,3,1,0:T(8,128)S(1)}) fusion(f32[16,2,1024]{2,1,0:T(2,128)S(1)} %fusion.17, pred[16,1024]{1,0:T(8,128)(4,1)S(1)} %broadcast_compare_fusion, bf16[16,1024,256]{2,1,0:T(8,128)(2,1)} %param.16, bf16[16,16,256]{2,1,0:T(8,128)(2,1)} %param.13), kind=kOutput, calls=%fused_computation.10 | convolution fusion | flops 136314368 | bytes 10766336 | tf_op jit(solution)/shard_map/uchd,ushd->uchs/dot_general | solution.py:35
  16.6 0.7 reshape.128
  17.3 4.3 %all-to-all-start = ((f32[4,1,128]{2,1,0:T(1,128)}), f32[4,1,128]{2,1,0:T(1,128)S(1)}, u32[]{:S(2)}, u32[]{:S(2)}) async-start(f32[4,1,128]{2,1,0:T(1,128)} %reshape.128), calls=%async_computation | async-start | bytes 4096 | tf_op jit(solution)/shard_map/all_to_all | solution.py:67
  21.5 0.7 fusion.11
  22.3 5.6 %fusion.13 = f32[1,16,16,2,128]{4,2,3,0,1:T(8,128)} fusion(f32[16,2,1024,16]{2,3,1,0:T(8,128)S(1)} %get-tuple-element.13, f32[16,16,2]{1,2,0:T(2,128)S(1)} %get-tuple-element.12, f32[16,2,1024]{2,1,0:T(2,128)S(1)} %fusion.17, pred[16,1024]{1,0:T(8,128)(4,1)S(1)} %broadcast_compare_fusion, bf16[16,1024,256]{2,1,0:T(8,128)(2,1)} %param.17), kind=kOutput, calls=%fused_computation.17 | convolution fusion | flops 136839168 | bytes 10897408 | tf_op jit(solution)/shard_map/uchs,ushd->uchd/dot_general | solution.py:54
  27.9 0.7 reshape.130
  28.6 3.3 %all-to-all-start.2 = ((f32[4,1,128]{2,1,0:T(1,128)}), f32[4,1,128]{2,1,0:T(1,128)S(1)}, u32[]{:S(2)}, u32[]{:S(2)}) async-start(f32[4,1,128]{2,1,0:T(1,128)} %reshape.130), calls=%async_computation.2 | async-start | bytes 4096 | tf_op jit(solution)/shard_map/all_to_all | solution.py:68
  31.8 0.8 %convert_multiply_fusion.1 = f32[4,16,256]{2,1,0:T(8,128)S(1)} fusion(bf16[16,16,256]{2,1,0:T(8,128)(2,1)} %param.14, s32[]{:T(128)S(6)} %select_n.14, bf16[16,16,256]{2,1,0:T(8,128)(2,1)} %param.13), kind=kLoop, calls=%fused_computation.44 | loop fusion | flops 49152 | bytes 131076 | tf_op jit(solution)/shard_map/mul | solution.py:88
  32.7 0.1 reduce_sum.45
  32.9 0.6 broadcast.73
  33.5 0.6 reduce.2
  34.2 1.3 %all-to-all-done.2 = f32[4,1,128]{2,1,0:T(1,128)S(1)} async-done(((f32[4,1,128]{2,1,0:T(1,128)}), f32[4,1,128]{2,1,0:T(1,128)S(1)}, u32[]{:S(2)}, u32[]{:S(2)}) %all-to-all-start.2) | async-done | bytes 2080 | tf_op jit(solution)/shard_map/all_to_all | solution.py:68
  35.6 3.4 %all-to-all-start.1 = ((f32[1,16,16,2,128]{4,2,3,0,1:T(8,128)}), f32[1,16,16,2,128]{4,2,3,0,1:T(8,128)S(1)}, u32[]{:S(2)}, u32[]{:S(2)}) async-start(f32[1,16,16,2,128]{4,2,3,0,1:T(8,128)} %fusion.13), calls=%async_computation.1 | async-start | bytes 524288 | tf_op jit(solution)/shard_map/all_to_all | solution.py:69
  39.0 0.6 reduce.1
  40.4 4.5 %all-to-all-done.1 = f32[1,16,16,2,128]{4,2,3,0,1:T(8,128)S(1)} async-done(((f32[1,16,16,2,128]{4,2,3,0,1:T(8,128)}), f32[1,16,16,2,128]{4,2,3,0,1:T(8,128)S(1)}, u32[]{:S(2)}, u32[]{:S(2)}) %all-to-all-start.1) | async-done | bytes 262176 | tf_op jit(solution)/shard_map/all_to_all | solution.py:69
  44.9 0.1 multiply_reduce_fusion
  45.1 0.9 %multiply_reduce_fusion.1 = (f32[4,16]{1,0:T(4,128)S(1)}, f32[4,16,256]{2,1,0:T(8,128)S(1)}) fusion(f32[4,16,256]{2,1,0:T(8,128)S(1)} %div.28, f32[4,16,256]{2,1,0:T(8,128)S(1)} %mul.129, bf16[16,16,256]{2,1,0:T(8,128)(2,1)} %param.15, s32[]{:T(128)S(6)} %select_n.14, f32[4,16,2,128]{3,1,2,0:T(8,128)S(1)} %multiply_reduce_fusion, f32[4,16,2]{1,2,0:T(2,128)S(1)} %copy.44), kind=kLoop, calls=%fused_computation.42 | loop fusion | flops 114624 | bytes 295684 | tf_op jit(solution)/shard_map/reduce_sum | solution.py:95
  46.0 1.7 %fusion.25 = f32[4,16,1024]{2,1,0:T(8,128)} fusion(bf16[256,1024]{1,0:T(8,128)(2,1)S(1)} %copy-done, f32[4,16,256]{2,1,0:T(8,128)S(1)} %get-tuple-element.6, bf16[16,16,256]{2,1,0:T(8,128)(2,1)} %param.23, s32[]{:T(128)S(6)} %select_n.14, f32[256]{0:T(256)S(1)} %copy-done.1), kind=kOutput, calls=%fused_computation.27 | convolution fusion | flops 33685504 | bytes 885764 | tf_op jit(solution)/shard_map/dot_general | solution.py:104
  47.7 12.4 %psum.7 = f32[4,16]{1,0:T(4,128)S(1)} all-reduce(f32[4,16]{1,0:T(4,128)S(1)} %get-tuple-element.5), channel_id=1, replica_groups=mesh['groups'=2,'seq'=4,'head'=4] {'head'}, use_global_device_ids=true, to_apply=%region_8.9 | all-reduce | flops 64 | bytes 512 | tf_op jit(solution)/shard_map/psum | solution.py:107
  60.1 8.5 %reduce-scatter.2.cloned.1.call-done = f32[4,16,256]{2,1,0:T(8,128)} async-done(((f32[4,16,1024]{2,1,0:T(8,128)}), f32[4,16,256]{2,1,0:T(8,128)}) %reduce-scatter.2.cloned.1.call-update) | async-done | bytes 65552 | tf_op jit(solution)/shard_map/reduce_scatter | solution.py:108
  68.6 1.5 %multiply_convert_fusion = bf16[4,16,256]{2,1,0:T(8,128)(2,1)} fusion(f32[4,16,256]{2,1,0:T(8,128)} %reduce-scatter.2.cloned.1.call-done, f32[4,16]{1,0:T(4,128)S(1)} %add_rsqrt_fusion), kind=kLoop, calls=%fused_computation.41 | loop fusion | flops 32768 | bytes 98560 | tf_op jit(solution)/shard_map/convert_element_type | solution.py:110
  (25 shorter events, 1.0 us)
Async XLA Ops:
  6.5 39.5 %copy-start = (bf16[256,1024]{1,0:T(8,128)(2,1)S(1)}, bf16[256,1024]{1,0:T(8,128)(2,1)}, u32[]{:S(2)}) copy-start(bf16[256,1024]{1,0:T(8,128)(2,1)} %param.25) | copy-start | bytes 1572868
  17.3 11.3 %all-to-all-start = ((f32[4,1,128]{2,1,0:T(1,128)}), f32[4,1,128]{2,1,0:T(1,128)S(1)}, u32[]{:S(2)}, u32[]{:S(2)}) async-start(f32[4,1,128]{2,1,0:T(1,128)} %reshape.128), calls=%async_computation | async-start | bytes 4096 | tf_op jit(solution)/shard_map/all_to_all | solution.py:67
  27.9 18.1 %copy-start.1 = (f32[256]{0:T(256)S(1)}, f32[256]{0:T(256)}, u32[]{:S(2)}) copy-start(f32[256]{0:T(256)} %param.24) | copy-start | bytes 3076
  28.6 7.0 %all-to-all-start.2 = ((f32[4,1,128]{2,1,0:T(1,128)}), f32[4,1,128]{2,1,0:T(1,128)S(1)}, u32[]{:S(2)}, u32[]{:S(2)}) async-start(f32[4,1,128]{2,1,0:T(1,128)} %reshape.130), calls=%async_computation.2 | async-start | bytes 4096 | tf_op jit(solution)/shard_map/all_to_all | solution.py:68
  35.6 9.4 %all-to-all-start.1 = ((f32[1,16,16,2,128]{4,2,3,0,1:T(8,128)}), f32[1,16,16,2,128]{4,2,3,0,1:T(8,128)S(1)}, u32[]{:S(2)}, u32[]{:S(2)}) async-start(f32[1,16,16,2,128]{4,2,3,0,1:T(8,128)} %fusion.13), calls=%async_computation.1 | async-start | bytes 524288 | tf_op jit(solution)/shard_map/all_to_all | solution.py:69
  39.0 29.6 %reduce-scatter.2.cloned.1.call-start = ((), (), s32[]{:S(2)}) async-start(), calls=%async_computation.4 | async-start | bytes 327680 | tf_op jit(solution)/shard_map/reduce_scatter | solution.py:108
Sparse Core Ops, SparseCore 0:
  47.8 20.6 reduce-scatter.1
where the time goes:
time: 77.7 us; the launch traced here: 77 us
  matrix products  16.5 us (21%)
  waiting for transfers between devices  14.3 us (18%)
  between operations  13.5 us (17%)
  blocking collectives  12.4 us (16%)
  starting transfers between devices  11 us (14%)
  other arithmetic  6.4 us (8%)
  local copies, waits for them, and re-layouts  2.82 us (4%)
    psum x1, blocking collectives, body(): squares = lax.psum(local_squares, 'head')  12.4 us
    reduce_scatter x1, waiting for transfers between devices, body(): lax.psum_scatter(partial_out, 'head', scatter_dimension=2, tiled=True)  8.48 us
    dot_general x1, matrix products, body(): jnp.einsum('uchd,ushd->uchs', query_heads, key_heads, preferred_element_t...  5.78 us
    dot_general x1, matrix products, body(): jnp.einsum('uchs,ushd->uchd', weights.astype(jnp.bfloat16), value_heads,...  5.58 us
    all_to_all x1, waiting for transfers between devices, body(): lax.all_to_all(block_acc[None], 'seq', split_axis=1, concat_axis=0, tiled...  4.5 us
    all_to_all x1, starting transfers between devices, body(): lax.all_to_all(block_max[None], 'seq', split_axis=1, concat_axis=0, tiled...  4.26 us
    all_to_all x1, starting transfers between devices, body(): lax.all_to_all(block_acc[None], 'seq', split_axis=1, concat_axis=0, tiled...  3.4 us
    all_to_all x1, starting transfers between devices, body(): lax.all_to_all(block_sum[None], 'seq', split_axis=1, concat_axis=0, tiled...  3.29 us
  transfers between devices with their start and end apart: 4, of which 3 were waited for; matrix products, arithmetic and copies ran while one was open for 14% of the time, Pallas kernels for 0%

commit v1 on v0

v1 whole, which is shorter than its diff:
```python
import functools
import math

import jax
import jax.numpy as jnp
from jax import lax
from jax.experimental import pallas as pl
from jax.experimental.pallas import tpu as pltpu
from jax.sharding import PartitionSpec as P

MESH = pl.DeviceIdType.MESH
LANES = 128
LOG2E = math.log2(math.e)
INVALID = -1e30
FLOOR = -1e29
NT = (((1,), (1,)), ((), ()))


def partner(rank, step, count):
    result, bit = 0, 1
    while bit < count:
        held = (rank // bit) % 2
        result = result + bit * (1 - held if (step // bit) % 2 else held)
        bit *= 2
    return result


def column_to_row(column, first, lanes):
    shape = (column.shape[0], lanes)
    row_id = lax.broadcasted_iota(jnp.int32, shape, 0)
    lane_id = lax.broadcasted_iota(jnp.int32, shape, 1)
    return jnp.sum(jnp.where(lane_id == row_id + first, column, 0.0), axis=0, keepdims=True)


def row_to_column(row, first, count):
    shape = (count, row.shape[1])
    row_id = lax.broadcasted_iota(jnp.int32, shape, 0)
    lane_id = lax.broadcasted_iota(jnp.int32, shape, 1)
    return jnp.sum(jnp.where(lane_id == row_id + first, row, 0.0), axis=1, keepdims=True)


def kernel(
    dims,
    len_ref,
    q_hbm,
    nk_hbm,
    nv_hbm,
    k_hbm,
    v_hbm,
    bucket_hbm,
    action_hbm,
    tb_hbm,
    ab_hbm,
    gate_hbm,
    gain_hbm,
    w_hbm,
    out_ref,
    q_s,
    nk_s,
    nv_s,
    k_s,
    v_s,
    bucket_s,
    action_s,
    tb_s,
    ab_s,
    gate_s,
    gain_s,
    w_s,
    bias_s,
    part_s,
    got_s,
    zpart_s,
    zgot_s,
    k_sem,
    v_sem,
    in_sem,
    late_sem,
    send_sem,
    recv_sem,
    zsend_sem,
    zrecv_sem,
):
    users, cands, block, heads, size, seqs, slices, local, out_cols = dims
    rows = heads * cands
    width = heads * size
    me = lax.axis_index("seq")
    mh = lax.axis_index("head")
    scale = LOG2E / math.sqrt(size)

    barrier = pltpu.get_barrier_semaphore()
    for step in range(1, seqs):
        pl.semaphore_signal(
            barrier, inc=1, device_id={"seq": partner(me, step, seqs)}, device_id_type=MESH
        )
    for step in range(1, slices):
        pl.semaphore_signal(
            barrier, inc=1, device_id={"head": (mh + step) % slices}, device_id_type=MESH
        )

    early = [
        pltpu.make_async_copy(source, target, in_sem.at[i])
        for i, (source, target) in enumerate(
            (
                (tb_hbm, tb_s),
                (ab_hbm, ab_s),
                (bucket_hbm, bucket_s),
                (action_hbm, action_s),
                (q_hbm, q_s),
            )
        )
    ]
    mine = pl.ds(me * local, local)
    late = [
        pltpu.make_async_copy(source, target, late_sem.at[i])
        for i, (source, target) in enumerate(
            (
                (nk_hbm.at[mine], nk_s),
                (nv_hbm.at[mine], nv_s),
                (gate_hbm.at[mine], gate_s),
                (gain_hbm, gain_s),
                (w_hbm, w_s),
            )
        )
    ]
    for copy in early:
        copy.start()
    order = []
    for turn in range(local):
        for step in range(seqs - 1, -1, -1):
            slot = len(order)
            user = partner(me, step, seqs) * local + turn
            k_copy = pltpu.make_async_copy(k_hbm.at[user], k_s.at[slot], k_sem.at[slot])
            v_copy = pltpu.make_async_copy(v_hbm.at[user], v_s.at[slot], v_sem.at[slot])
            k_copy.start()
            v_copy.start()
            order.append((turn, step, user, k_copy, v_copy))
        if turn == 0:
            for copy in late:
                copy.start()

    for copy in early:
        copy.wait()

    def table(ref, head):
        count = ref.shape[0]
        return column_to_row(ref[:, head : head + 1] * LOG2E, 0, LANES)

    for head in range(heads):
        tb_row = jnp.broadcast_to(table(tb_s, head), (users, LANES))
        ab_row = jnp.broadcast_to(table(ab_s, head), (users, LANES))
        for chunk in range(block // LANES):
            lanes = slice(chunk * LANES, (chunk + 1) * LANES)
            bias_s[head, :, lanes] = jnp.take_along_axis(
                tb_row, bucket_s[:, lanes], axis=1
            ) + jnp.take_along_axis(ab_row, action_s[:, lanes], axis=1)

    position = me * block + lax.broadcasted_iota(jnp.int32, (1, block), 1)
    lane_of = lax.broadcasted_iota(jnp.int32, (cands, width), 1)

    def split_query(query):
        return jnp.concatenate(
            [
                jnp.where(lane_of // size == head, query, jnp.zeros_like(query))
                for head in range(heads)
            ],
            axis=0,
        )

    def attend(slot):
        turn, step, user, _, _ = order[slot]
        raw = lax.dot_general(
            split_query(q_s[user]), k_s[slot], NT, preferred_element_type=jnp.float32
        )
        valid = position < len_ref[user]
        bias = jnp.concatenate(
            [
                jnp.broadcast_to(
                    jnp.where(valid, bias_s[head, pl.ds(user, 1), :], INVALID), (cands, block)
                )
                for head in range(heads)
            ],
            axis=0,
        )
        scores = raw * scale + bias
        top = jnp.maximum(jnp.max(scores, axis=1, keepdims=True), FLOOR)
        weights = jnp.exp2(scores - top)
        total = jnp.sum(weights, axis=1, keepdims=True)
        mixed = jnp.dot(
            weights.astype(jnp.bfloat16), v_s[slot], preferred_element_type=jnp.float32
        )
        for head in range(heads):
            held = slice(head * cands, (head + 1) * cands)
            part_s[turn, step, held, :] = mixed[held, head * size : (head + 1) * size]
        stats = column_to_row(top, 0, size) + column_to_row(total, rows, size)
        part_s[turn, step, rows : rows + 8, :] = jnp.broadcast_to(stats, (8, size))

    def exchange(turn, step):
        return pltpu.make_async_remote_copy(
            src_ref=part_s.at[turn, step],
            dst_ref=got_s.at[turn, step - 1],
            send_sem=send_sem.at[turn, step - 1],
            recv_sem=recv_sem.at[turn, step - 1],
            device_id={"seq": partner(me, step, seqs)},
            device_id_type=MESH,
        )

    def spread(turn, step):
        target = (mh + step) % slices
        return pltpu.make_async_remote_copy(
            src_ref=zpart_s.at[turn, target],
            dst_ref=zgot_s.at[turn, step - 1],
            send_sem=zsend_sem.at[turn, step - 1],
            recv_sem=zrecv_sem.at[turn, step - 1],
            device_id={"head": target},
            device_id_type=MESH,
        )

    def combine(turn):
        for step in range(1, seqs):
            exchange(turn, step).wait_recv()
        blocks = [part_s.at[turn, 0]] + [got_s.at[turn, step - 1] for step in range(1, seqs)]
        query = q_s[me * local + turn].astype(jnp.float32)
        new_key = nk_s[turn].astype(jnp.float32)
        new_value = nv_s[turn].astype(jnp.float32)
        product = query * new_key

        def by_head(source):
            return jnp.concatenate(
                [source[:, head * size : (head + 1) * size] for head in range(heads)], axis=0
            )

        own = jnp.sum(by_head(product), axis=1, keepdims=True) * scale
        maxima = [row_to_column(ref[rows : rows + 1, :], 0, rows) for ref in blocks]
        sums = [row_to_column(ref[rows : rows + 1, :], rows, rows) for ref in blocks]
        top = functools.reduce(jnp.maximum, maxima, own)
        own_factor = jnp.exp2(own - top)
        numer = own_factor * by_head(new_value)
        denom = own_factor
        for ref, high, amount in zip(blocks, maxima, sums):
            factor = jnp.exp2(high - top)
            numer = numer + factor * ref[:rows, :]
            denom = denom + factor * amount
        attended = numer / denom
        squares = jnp.sum(jnp.square(attended), axis=1, keepdims=True)
        square = squares[:cands]
        for head in range(1, heads):
            square = square + squares[head * cands : (head + 1) * cands]
        wide = jnp.concatenate(
            [attended[head * cands : (head + 1) * cands] for head in range(heads)], axis=1
        )
        gate = gate_s[turn].astype(jnp.float32)
        gain = gain_s[...].reshape(1, width)
        hidden = (wide * gain * (gate / (1.0 + jnp.exp(-gate)))).astype(jnp.bfloat16)
        projected = jnp.dot(hidden, w_s[...], preferred_element_type=jnp.float32)
        square_row = jnp.broadcast_to(column_to_row(square, 0, out_cols), (8, out_cols))
        for target in range(slices):
            zpart_s[turn, target, :cands, :] = projected[
                :, target * out_cols : (target + 1) * out_cols
            ]
            zpart_s[turn, target, cands : cands + 8, :] = square_row
        for step in range(1, slices):
            spread(turn, step).start()

    def finish(turn):
        total = zpart_s[turn, mh]
        for step in range(1, slices):
            spread(turn, step).wait_recv()
            total = total + zgot_s[turn, step - 1]
        square = row_to_column(total[cands : cands + 1, :], 0, cands)
        factor = 1.0 / jnp.sqrt(square / (width * slices) + 1e-6)
        out_ref[turn] = (total[:cands] * factor).astype(out_ref.dtype)

    for turn in range(local):
        for step in range(seqs - 1, -1, -2):
            slots = [turn * seqs + seqs - 1 - step]
            if step:
                slots.append(slots[0] + 1)
            for slot in slots:
                order[slot][3].wait()
                order[slot][4].wait()
            for slot in slots:
                attend(slot)
            if turn == 0 and step == seqs - 1:
                pl.semaphore_wait(barrier, seqs - 1 + slices - 1)
            for slot in slots:
                if order[slot][1]:
                    exchange(turn, order[slot][1]).start()
        if turn == 0:
            for copy in late:
                copy.wait()
        else:
            combine(turn - 1)
    combine(local - 1)
    for turn in range(local):
        finish(turn)
    for turn in range(local):
        for step in range(1, seqs):
            exchange(turn, step).wait_send()
        for step in range(1, slices):
            spread(turn, step).wait_send()


def body(
    query,
    new_key,
    new_value,
    keys,
    values,
    lengths,
    time_bucket,
    action,
    time_bias,
    action_bias,
    gate,
    norm_gain,
    w_out,
):
    users, block, width = keys.shape
    cands = query.shape[1]
    heads = time_bias.shape[1]
    size = width // heads
    seqs = lax.axis_size("seq")
    slices = lax.axis_size("head")
    local = users // seqs
    rows = heads * cands
    out_cols = w_out.shape[1] // slices
    dims = (users, cands, block, heads, size, seqs, slices, local, out_cols)
    f32, bf16 = jnp.float32, jnp.bfloat16
    anywhere = pl.BlockSpec(memory_space=pl.ANY)
    return pl.pallas_call(
        functools.partial(kernel, dims),
        out_shape=jax.ShapeDtypeStruct((local, cands, out_cols), bf16),
        in_specs=[pl.BlockSpec(memory_space=pltpu.SMEM)] + [anywhere] * 12,
        out_specs=pl.BlockSpec(memory_space=pltpu.VMEM),
        scratch_shapes=[
            pltpu.VMEM((users, cands, width), bf16),
            pltpu.VMEM((local, cands, width), bf16),
            pltpu.VMEM((local, cands, width), bf16),
            pltpu.VMEM((users, block, width), bf16),
            pltpu.VMEM((users, block, width), bf16),
            pltpu.VMEM((users, block), jnp.int32),
            pltpu.VMEM((users, block), jnp.int32),
            pltpu.VMEM(time_bias.shape, f32),
            pltpu.VMEM(action_bias.shape, f32),
            pltpu.VMEM((local, cands, width), bf16),
            pltpu.VMEM((width,), f32),
            pltpu.VMEM(w_out.shape, bf16),
            pltpu.VMEM((heads, users, block), f32),
            pltpu.VMEM((local, seqs, rows + 8, size), f32),
            pltpu.VMEM((local, seqs - 1, rows + 8, size), f32),
            pltpu.VMEM((local, slices, cands + 8, out_cols), f32),
            pltpu.VMEM((local, slices - 1, cands + 8, out_cols), f32),
            pltpu.SemaphoreType.DMA((users,)),
            pltpu.SemaphoreType.DMA((users,)),
            pltpu.SemaphoreType.DMA((5,)),
            pltpu.SemaphoreType.DMA((5,)),
            pltpu.SemaphoreType.DMA((local, seqs - 1)),
            pltpu.SemaphoreType.DMA((local, seqs - 1)),
            pltpu.SemaphoreType.DMA((local, slices - 1)),
            pltpu.SemaphoreType.DMA((local, slices - 1)),
        ],
        compiler_params=pltpu.CompilerParams(
            collective_id=0, has_side_effects=True, vmem_limit_bytes=48 * 1024 * 1024
        ),
    )(
        lengths,
        query,
        new_key,
        new_value,
        keys,
        values,
        time_bucket,
        action,
        time_bias,
        action_bias,
        gate,
        norm_gain,
        w_out,
    )


def solution(mesh):
    placed = (
        P("groups", None, "head"),
        P("groups", None, "head"),
        P("groups", None, "head"),
        P("groups", "seq", "head"),
        P("groups", "seq", "head"),
        P("groups"),
        P("groups", "seq"),
        P("groups", "seq"),
        P(None, "head"),
        P(None, "head"),
        P("groups", None, "head"),
        P("head"),
        P("head", None),
    )
    return jax.shard_map(
        body,
        mesh=mesh,
        in_specs=placed,
        out_specs=P(("groups", "seq"), None, "head"),
        check_vma=False,
    )
```

time: 77.7 us -> 32.1 us (0.41)
  Pallas kernels: 0 us -> 21.9 us
  matrix products: 16.5 us -> 0 us
  waiting for transfers between devices: 14.3 us -> 0 us
  between operations: 13.5 us -> 0.02 us
  blocking collectives: 12.4 us -> 0 us
  starting transfers between devices: 11 us -> 0 us
  local copies, waits for them, and re-layouts: 2.82 us -> 9.81 us
  other arithmetic: 6.4 us -> 0 us
    pallas_call x0 -> x1, Pallas kernels: none -> 21.9 us  [body(): pl.pallas_call(functools.partial(kernel, dims), out_shape=jax.ShapeDtypeS...]
    dot_general x5 -> x0, matrix products: 16.5 us -> none  [the longest x1 5.78 us: body(): jnp.einsum('uchd,ushd->uchs', query_heads, key_heads, preferred_element_t...]
    psum x1 -> x0, blocking collectives: 12.4 us -> none  [body(): squares = lax.psum(local_squares, 'head')]
    all_to_all x3 -> x0, starting transfers between devices: 11 us -> none  [the longest x1 4.26 us: body(): lax.all_to_all(block_max[None], 'seq', split_axis=1, concat_axis=0, tiled...]
    reduce_scatter x1 -> x0, waiting for transfers between devices: 8.48 us -> none  [body(): lax.psum_scatter(partial_out, 'head', scatter_dimension=2, tiled=True)]
    unnamed x10 -> x21, local copies, waits for them, and re-layouts: 1.54 us -> 9.81 us
    all_to_all x3 -> x0, waiting for transfers between devices: 5.82 us -> none  [the longest x1 4.5 us: body(): lax.all_to_all(block_acc[None], 'seq', split_axis=1, concat_axis=0, tiled...]
    reduce_sum x5 -> x0, other arithmetic: 1.98 us -> none  [the longest x1 0.93 us: body(): local_squares = jnp.sum(jnp.square(attended), axis=(2, 3))]
  transfers between devices with their start and end apart: 4 -> 0, of which waited for: 3 -> 0; matrix products, arithmetic and copies ran while one was open for 14% -> 0% of each run, Pallas kernels for 0% -> 0%
where the time goes in v1:
time: 32.1 us; the launch traced here: 31.7 us
  Pallas kernels  21.9 us (68%)
  local copies, waits for them, and re-layouts  9.81 us (31%)
    pallas_call x1, Pallas kernels, body(): pl.pallas_call(functools.partial(kernel, dims), out_shape=jax.ShapeDtypeS...  21.9 us
    unnamed x21, local copies, waits for them, and re-layouts  9.81 us

profile of v1, /device:TPU:0, one launch (start us, length us, event | category | flops | bytes accessed | tf_op | source)
XLA Modules:
  0.0 31.7 jit_solution(1513504340892096143)
XLA Ops:
  0.0 0.8 %copy.15.ab_hbm = f32[16,2]{1,0:T(8,128)S(1)} copy(f32[16,2]{0,1:T(2,128)} %param.22) | data formatting | bytes 256 | tf_op args[9]
  0.8 0.8 %copy.14.tb_hbm = f32[64,2]{1,0:T(8,128)S(1)} copy(f32[64,2]{0,1:T(2,128)} %param.21) | data formatting | bytes 1024 | tf_op args[8]
  1.5 0.0 copy-start
  1.5 1.0 %copy-done = bf16[256,1024]{1,0:T(8,128)(2,1)S(1)} copy-done((bf16[256,1024]{1,0:T(8,128)(2,1)S(1)}, bf16[256,1024]{1,0:T(8,128)(2,1)}, u32[]{:S(2)}) %copy-start) | copy-done | bytes 524312
  2.6 0.0 copy-start.1
  2.6 0.9 %copy-done.1 = bf16[16,16,256]{2,1,0:T(8,128)(2,1)S(1)} copy-done((bf16[16,16,256]{2,1,0:T(8,128)(2,1)S(1)}, bf16[16,16,256]{2,1,0:T(8,128)(2,1)}, u32[]{:S(2)}) %copy-start.1) | copy-done | bytes 131096
  3.5 0.0 copy-start.2
  3.5 0.9 %copy-done.2 = bf16[16,16,256]{2,1,0:T(8,128)(2,1)S(1)} copy-done((bf16[16,16,256]{2,1,0:T(8,128)(2,1)S(1)}, bf16[16,16,256]{2,1,0:T(8,128)(2,1)}, u32[]{:S(2)}) %copy-start.2) | copy-done | bytes 131096
  4.4 0.0 copy-start.3
  4.4 0.9 %copy-done.3 = bf16[16,16,256]{2,1,0:T(8,128)(2,1)S(1)} copy-done((bf16[16,16,256]{2,1,0:T(8,128)(2,1)S(1)}, bf16[16,16,256]{2,1,0:T(8,128)(2,1)}, u32[]{:S(2)}) %copy-start.3) | copy-done | bytes 131096
  5.3 0.0 copy-start.4
  5.3 0.9 %copy-done.4 = bf16[16,16,256]{2,1,0:T(8,128)(2,1)S(1)} copy-done((bf16[16,16,256]{2,1,0:T(8,128)(2,1)S(1)}, bf16[16,16,256]{2,1,0:T(8,128)(2,1)}, u32[]{:S(2)}) %copy-start.4) | copy-done | bytes 131096
  6.2 0.0 copy-start.5
  6.2 0.8 %copy-done.5 = s32[16,1024]{1,0:T(8,128)S(1)} copy-done((s32[16,1024]{1,0:T(8,128)S(1)}, s32[16,1024]{1,0:T(8,128)}, u32[]{:S(2)}) %copy-start.5) | copy-done | bytes 65560
  7.0 0.0 copy-start.6
  7.0 0.8 %copy-done.6 = s32[16,1024]{1,0:T(8,128)S(1)} copy-done((s32[16,1024]{1,0:T(8,128)S(1)}, s32[16,1024]{1,0:T(8,128)}, u32[]{:S(2)}) %copy-start.6) | copy-done | bytes 65560
  7.9 0.0 copy-start.7
  7.9 0.7 %copy-done.7 = f32[256]{0:T(256)S(1)} copy-done((f32[256]{0:T(256)S(1)}, f32[256]{0:T(256)}, u32[]{:S(2)}) %copy-start.7) | copy-done | bytes 1048
  8.5 0.0 copy-start.8
  8.5 0.7 %copy-done.8 = s32[16]{0:T(128)S(1)} copy-done((s32[16]{0:T(128)S(1)}, s32[16]{0:T(128)}, u32[]{:S(2)}) %copy-start.8) | copy-done | bytes 88
  9.2 21.9 %shard_map.127 = bf16[4,16,256]{2,1,0:T(8,128)(2,1)S(1)} custom-call(s32[16]{0:T(128)S(1)} %copy-done.8, bf16[16,16,256]{2,1,0:T(8,128)(2,1)S(1)} %copy-done.1, bf16[16,16,256]{2,1,0:T(8,128)(2,1)S(1)} %copy-done.2, bf16[16,16,256]{2,1,0:T(8,128)(2,1)S(1)} %copy-done.3, bf16[16,1024,256]{2,1,0:T(8,128)(2,1)} %k_hbm.1, bf16[16,1024,256]{2,1,0:T(8,128)(2,1)} %v_hbm.1, ...), custom_call_target="tpu_custom_call" | custom-call | tf_op jit(solution)/shard_map/pallas_call | solution.py:331
  31.1 0.6 %copy.17 = bf16[4,16,256]{2,1,0:T(8,128)(2,1)} copy(bf16[4,16,256]{2,1,0:T(8,128)(2,1)S(1)} %shard_map.127) | data formatting | bytes 65536
Async XLA Ops:
  1.5 1.0 %copy-start = (bf16[256,1024]{1,0:T(8,128)(2,1)S(1)}, bf16[256,1024]{1,0:T(8,128)(2,1)}, u32[]{:S(2)}) copy-start(bf16[256,1024]{1,0:T(8,128)(2,1)} %w_hbm.1) | copy-start | bytes 1572868
  2.6 0.9 %copy-start.1 = (bf16[16,16,256]{2,1,0:T(8,128)(2,1)S(1)}, bf16[16,16,256]{2,1,0:T(8,128)(2,1)}, u32[]{:S(2)}) copy-start(bf16[16,16,256]{2,1,0:T(8,128)(2,1)} %q_hbm.1) | copy-start | bytes 393220
  3.5 0.9 %copy-start.2 = (bf16[16,16,256]{2,1,0:T(8,128)(2,1)S(1)}, bf16[16,16,256]{2,1,0:T(8,128)(2,1)}, u32[]{:S(2)}) copy-start(bf16[16,16,256]{2,1,0:T(8,128)(2,1)} %nk_hbm.1) | copy-start | bytes 393220
  4.4 0.9 %copy-start.3 = (bf16[16,16,256]{2,1,0:T(8,128)(2,1)S(1)}, bf16[16,16,256]{2,1,0:T(8,128)(2,1)}, u32[]{:S(2)}) copy-start(bf16[16,16,256]{2,1,0:T(8,128)(2,1)} %nv_hbm.1) | copy-start | bytes 393220
  5.3 0.9 %copy-start.4 = (bf16[16,16,256]{2,1,0:T(8,128)(2,1)S(1)}, bf16[16,16,256]{2,1,0:T(8,128)(2,1)}, u32[]{:S(2)}) copy-start(bf16[16,16,256]{2,1,0:T(8,128)(2,1)} %gate_hbm.1) | copy-start | bytes 393220
  6.2 0.8 %copy-start.5 = (s32[16,1024]{1,0:T(8,128)S(1)}, s32[16,1024]{1,0:T(8,128)}, u32[]{:S(2)}) copy-start(s32[16,1024]{1,0:T(8,128)} %bucket_hbm.1) | copy-start | bytes 196612
  7.0 0.8 %copy-start.6 = (s32[16,1024]{1,0:T(8,128)S(1)}, s32[16,1024]{1,0:T(8,128)}, u32[]{:S(2)}) copy-start(s32[16,1024]{1,0:T(8,128)} %action_hbm.1) | copy-start | bytes 196612
  7.9 0.7 %copy-start.7 = (f32[256]{0:T(256)S(1)}, f32[256]{0:T(256)}, u32[]{:S(2)}) copy-start(f32[256]{0:T(256)} %gain_hbm.1) | copy-start | bytes 3076
  8.5 0.7 %copy-start.8 = (s32[16]{0:T(128)S(1)}, s32[16]{0:T(128)}, u32[]{:S(2)}) copy-start(s32[16]{0:T(128)} %len_ref.1) | copy-start | bytes 196

commit v2 on v1

--- a/solution.py
+++ b/solution.py
@@ -11,6 +11,7 @@
 MESH = pl.DeviceIdType.MESH
 LANES = 128
 LOG2E = math.log2(math.e)
+AHEAD = 4
 INVALID = -1e30
 FLOOR = -1e29
 NT = (((1,), (1,)), ((), ()))
@@ -41,7 +42,7 @@
 
 def kernel(
     dims,
-    len_ref,
+    len_hbm,
     q_hbm,
     nk_hbm,
     nv_hbm,
@@ -55,6 +56,7 @@
     gain_hbm,
     w_hbm,
     out_ref,
+    len_ref,
     q_s,
     nk_s,
     nv_s,
@@ -72,6 +74,8 @@
     got_s,
     zpart_s,
     zgot_s,
+    square_s,
+    squares_s,
     k_sem,
     v_sem,
     in_sem,
@@ -80,6 +84,8 @@
     recv_sem,
     zsend_sem,
     zrecv_sem,
+    tsend_sem,
+    trecv_sem,
 ):
     users, cands, block, heads, size, seqs, slices, local, out_cols = dims
     rows = heads * cands
@@ -102,6 +108,7 @@
         pltpu.make_async_copy(source, target, in_sem.at[i])
         for i, (source, target) in enumerate(
             (
+                (len_hbm, len_ref),
                 (tb_hbm, tb_s),
                 (ab_hbm, ab_s),
                 (bucket_hbm, bucket_s),
@@ -132,19 +139,23 @@
             user = partner(me, step, seqs) * local + turn
             k_copy = pltpu.make_async_copy(k_hbm.at[user], k_s.at[slot], k_sem.at[slot])
             v_copy = pltpu.make_async_copy(v_hbm.at[user], v_s.at[slot], v_sem.at[slot])
-            k_copy.start()
-            v_copy.start()
             order.append((turn, step, user, k_copy, v_copy))
-        if turn == 0:
-            for copy in late:
-                copy.start()
-
+
+    def fetch(slot):
+        if slot < users:
+            order[slot][3].start()
+            order[slot][4].start()
+
+    for slot in range(AHEAD):
+        fetch(slot)
+
+    square_s[...] = jnp.zeros_like(square_s)
     for copy in early:
         copy.wait()
 
     def table(ref, head):
-        count = ref.shape[0]
-        return column_to_row(ref[:, head : head + 1] * LOG2E, 0, LANES)
+        row = ref[head : head + 1, :] * LOG2E
+        return jnp.concatenate([row, jnp.zeros((1, LANES - row.shape[1]), row.dtype)], axis=1)
 
     for head in range(heads):
         tb_row = jnp.broadcast_to(table(tb_s, head), (users, LANES))
@@ -213,6 +224,16 @@
             send_sem=zsend_sem.at[turn, step - 1],
             recv_sem=zrecv_sem.at[turn, step - 1],
             device_id={"head": target},
+            device_id_type=MESH,
+        )
+
+    def tell(step):
+        return pltpu.make_async_remote_copy(
+            src_ref=square_s,
+            dst_ref=squares_s.at[step - 1],
+            send_sem=tsend_sem.at[step - 1],
+            recv_sem=trecv_sem.at[step - 1],
+            device_id={"head": (mh + step) % slices},
             device_id_type=MESH,
         )
 
@@ -246,6 +267,10 @@
         square = squares[:cands]
         for head in range(1, heads):
             square = square + squares[head * cands : (head + 1) * cands]
+        square_s[turn : turn + 1, :] = column_to_row(square, 0, LANES)
+        if turn == local - 1:
+            for step in range(1, slices):
+                tell(step).start()
         wide = jnp.concatenate(
             [attended[head * cands : (head + 1) * cands] for head in range(heads)], axis=1
         )
@@ -253,13 +278,9 @@
         gain = gain_s[...].reshape(1, width)
         hidden = (wide * gain * (gate / (1.0 + jnp.exp(-gate)))).astype(jnp.bfloat16)
         projected = jnp.dot(hidden, w_s[...], preferred_element_type=jnp.float32)
-        square_row = jnp.broadcast_to(column_to_row(square, 0, out_cols), (8, out_cols))
         for target in range(slices):
-            zpart_s[turn, target, :cands, :] = projected[
-                :, target * out_cols : (target + 1) * out_cols
-            ]
-            zpart_s[turn, target, cands : cands + 8, :] = square_row
-        for step in range(1, slices):
+            zpart_s[turn, target] = projected[:, target * out_cols : (target + 1) * out_cols]
+        for step in range(slices - 1, 0, -1):
             spread(turn, step).start()
 
     def finish(turn):
@@ -267,9 +288,7 @@
         for step in range(1, slices):
             spread(turn, step).wait_recv()
             total = total + zgot_s[turn, step - 1]
-        square = row_to_column(total[cands : cands + 1, :], 0, cands)
-        factor = 1.0 / jnp.sqrt(square / (width * slices) + 1e-6)
-        out_ref[turn] = (total[:cands] * factor).astype(out_ref.dtype)
+        out_ref[turn] = (total * factor_of(turn)).astype(out_ref.dtype)
 
     for turn in range(local):
         for step in range(seqs - 1, -1, -2):
@@ -280,20 +299,40 @@
                 order[slot][3].wait()
                 order[slot][4].wait()
             for slot in slots:
+                fetch(slot + AHEAD)
+            if turn == 0 and step == seqs - 1:
+                for copy in late:
+                    copy.start()
+            for slot in slots:
                 attend(slot)
             if turn == 0 and step == seqs - 1:
                 pl.semaphore_wait(barrier, seqs - 1 + slices - 1)
             for slot in slots:
                 if order[slot][1]:
                     exchange(turn, order[slot][1]).start()
-        if turn == 0:
-            for copy in late:
-                copy.wait()
-        else:
-            combine(turn - 1)
+            if turn > 0 and step == seqs - 1:
+                if turn == 1:
+                    for copy in late:
+                        copy.wait()
+                combine(turn - 1)
+    if local == 1:
+        for copy in late:
+            copy.wait()
     combine(local - 1)
+    for step in range(1, slices):
+        tell(step).wait_recv()
+    square = square_s[...]
+    for step in range(1, slices):
+        square = square + squares_s[step - 1]
+
+    def factor_of(turn):
+        column = row_to_column(square[turn : turn + 1, :], 0, cands)
+        return 1.0 / jnp.sqrt(column / (width * slices) + 1e-6)
+
     for turn in range(local):
         finish(turn)
+    for step in range(1, slices):
+        tell(step).wait_send()
     for turn in range(local):
         for step in range(1, seqs):
             exchange(turn, step).wait_send()
@@ -324,16 +363,18 @@
     slices = lax.axis_size("head")
     local = users // seqs
     rows = heads * cands
+    lines = -(-local // 8) * 8
     out_cols = w_out.shape[1] // slices
     dims = (users, cands, block, heads, size, seqs, slices, local, out_cols)
     f32, bf16 = jnp.float32, jnp.bfloat16
-    anywhere = pl.BlockSpec(memory_space=pl.ANY)
+    anywhere = pl.BlockSpec(memory_space=pltpu.HBM)
     return pl.pallas_call(
         functools.partial(kernel, dims),
         out_shape=jax.ShapeDtypeStruct((local, cands, out_cols), bf16),
-        in_specs=[pl.BlockSpec(memory_space=pltpu.SMEM)] + [anywhere] * 12,
+        in_specs=[anywhere] * 13,
         out_specs=pl.BlockSpec(memory_space=pltpu.VMEM),
         scratch_shapes=[
+            pltpu.SMEM((users,), jnp.int32),
             pltpu.VMEM((users, cands, width), bf16),
             pltpu.VMEM((local, cands, width), bf16),
             pltpu.VMEM((local, cands, width), bf16),
@@ -341,27 +382,31 @@
             pltpu.VMEM((users, block, width), bf16),
             pltpu.VMEM((users, block), jnp.int32),
             pltpu.VMEM((users, block), jnp.int32),
-            pltpu.VMEM(time_bias.shape, f32),
-            pltpu.VMEM(action_bias.shape, f32),
+            pltpu.VMEM(time_bias.T.shape, f32),
+            pltpu.VMEM(action_bias.T.shape, f32),
             pltpu.VMEM((local, cands, width), bf16),
             pltpu.VMEM((width,), f32),
             pltpu.VMEM(w_out.shape, bf16),
             pltpu.VMEM((heads, users, block), f32),
             pltpu.VMEM((local, seqs, rows + 8, size), f32),
             pltpu.VMEM((local, seqs - 1, rows + 8, size), f32),
-            pltpu.VMEM((local, slices, cands + 8, out_cols), f32),
-            pltpu.VMEM((local, slices - 1, cands + 8, out_cols), f32),
+            pltpu.VMEM((local, slices, cands, out_cols), f32),
+            pltpu.VMEM((local, slices - 1, cands, out_cols), f32),
+            pltpu.VMEM((lines, LANES), f32),
+            pltpu.VMEM((slices - 1, lines, LANES), f32),
             pltpu.SemaphoreType.DMA((users,)),
             pltpu.SemaphoreType.DMA((users,)),
-            pltpu.SemaphoreType.DMA((5,)),
+            pltpu.SemaphoreType.DMA((6,)),
             pltpu.SemaphoreType.DMA((5,)),
             pltpu.SemaphoreType.DMA((local, seqs - 1)),
             pltpu.SemaphoreType.DMA((local, seqs - 1)),
             pltpu.SemaphoreType.DMA((local, slices - 1)),
             pltpu.SemaphoreType.DMA((local, slices - 1)),
+            pltpu.SemaphoreType.DMA((slices - 1,)),
+            pltpu.SemaphoreType.DMA((slices - 1,)),
         ],
         compiler_params=pltpu.CompilerParams(
-            collective_id=0, has_side_effects=True, vmem_limit_bytes=48 * 1024 * 1024
+            collective_id=0, has_side_effects=True, vmem_limit_bytes=67043328
         ),
     )(
         lengths,
@@ -372,8 +417,8 @@
         values,
         time_bucket,
         action,
-        time_bias,
-        action_bias,
+        time_bias.T,
+        action_bias.T,
         gate,
         norm_gain,
         w_out,

time: 32.1 us -> 24.7 us (0.77)
  local copies, waits for them, and re-layouts: 9.81 us -> 1.38 us
  Pallas kernels: 21.9 us -> 23.1 us
    unnamed x21 -> x1, local copies, waits for them, and re-layouts: 9.81 us -> 1.38 us
    pallas_call x1, Pallas kernels: 21.9 us -> 23.1 us  [body(): pl.pallas_call(functools.partial(kernel, dims), out_shape=jax.ShapeDtypeS...]
where the time goes in v2:
time: 24.7 us; the launch traced here: 24.5 us
  Pallas kernels  23.1 us (94%)
  local copies, waits for them, and re-layouts  1.38 us (6%)
    pallas_call x1, Pallas kernels, body(): pl.pallas_call(functools.partial(kernel, dims), out_shape=jax.ShapeDtypeS...  23.1 us
    unnamed x1, local copies, waits for them, and re-layouts  1.38 us

profile of v2, /device:TPU:0, one launch (start us, length us, event | category | flops | bytes accessed | tf_op | source)
XLA Modules:
  0.0 24.5 jit_solution(10378261460086923789)
XLA Ops:
  0.0 23.1 %shard_map.127 = bf16[4,16,256]{2,1,0:T(8,128)(2,1)} custom-call(s32[16]{0:T(128)} %len_hbm.1, bf16[16,16,256]{2,1,0:T(8,128)(2,1)} %q_hbm.1, bf16[16,16,256]{2,1,0:T(8,128)(2,1)} %nk_hbm.1, bf16[16,16,256]{2,1,0:T(8,128)(2,1)} %nv_hbm.1, bf16[16,1024,256]{2,1,0:T(8,128)(2,1)} %k_hbm.1, bf16[16,1024,256]{2,1,0:T(8,128)(2,1)} %v_hbm.1, ...), custom_call_target="tpu_custom_call" | custom-call | tf_op jit(solution)/shard_map/pallas_call | solution.py:371
  23.1 1.4 %copy.15 = bf16[4,16,256]{2,1,0:T(8,128)(2,1)} copy(bf16[4,16,256]{2,1,0:T(8,128)(2,1)} %shard_map.127) | data formatting | bytes 65536
